TPU v7x, 256 devices: a whole 4x4x8 slice. The times are simulated.
256 devices in a mesh: outer: 8 (over x, y_hi), dp: 32 (over y_lo, z, core).
Axes of the slice: x: 4, y: 4 (y_hi: 2, y_lo: 2; y = y_hi * 2 + y_lo), z: 8, core: 2. Of those that a mesh axis runs over, the one named last changes fastest.
Arguments:
- fast_weights: float32 [8, 4096, 2048], P('outer', 'dp'), may hold values from -6 to 6
- slow_weights: float32 [4096, 2048], P('dp', 'outer'), may hold values from -6 to 6
- momentum: float32 [4096, 2048], P('dp', 'outer'), may hold values from -3 to 3
- tokens: bfloat16 [196608, 4096], P(('outer', 'dp')), may hold values from -6 to 6
- norm_gain: float32 [4096], replicated, may hold values from 0.1 to 1.9
Outputs:
- slow_next: float32 [4096, 2048], P('dp', 'outer')
- momentum_next: float32 [4096, 2048], P('dp', 'outer')
- fast_next: float32 [4096, 2048], P('dp')
- key_values: bfloat16 [196608, 2048], P(('outer', 'dp'))
All inputs are finite; a program needn't handle non-finite values.
Results may differ from a plain program's by a relative error of at most 0.0057.
Values may be sent and summed in bfloat16 or wider, within the bound.
A program may use at most 128 MiB of HBM per device.

v0:
```python
import jax
import jax.numpy as jnp
from jax import lax
from jax.sharding import PartitionSpec as P

OUTER_LR = 0.7
MOMENTUM_COEF = 0.9
EPSILON = 1e-05


def cut_along(shard, dim, size):
    before, after = (shard.shape[:dim], shard.shape[dim + 1 :])
    return jnp.moveaxis(shard.reshape(*before, size, -1, *after), dim, 0)


def summed_on_arrival(shard, axis, dim):
    parts = cut_along(shard, dim, lax.axis_size(axis))
    arrived = lax.all_to_all(parts, axis, split_axis=0, concat_axis=0, tiled=True)
    return arrived.sum(axis=0)


def in_order(parts, dim):
    lengths = list(parts.shape[1:])
    lengths[dim] *= parts.shape[0]
    return jnp.moveaxis(parts, 0, dim).reshape(lengths)


def sent_to_all(shard, axis):
    copies = jnp.broadcast_to(shard, (lax.axis_size(axis), *shard.shape))
    return lax.all_to_all(copies, axis, split_axis=0, concat_axis=0, tiled=True)


def collect(shard, axis, dim):
    return in_order(sent_to_all(shard, axis), dim)


def outer_update(slow_part, moment_part, fast_total, pod_count):
    outer_grad = slow_part - fast_total / pod_count
    moment_next = MOMENTUM_COEF * moment_part + outer_grad
    slow_next = slow_part - OUTER_LR * (outer_grad + MOMENTUM_COEF * moment_next)
    return (slow_next, moment_next)


def body(fast_weights, slow_weights, momentum, tokens, norm_gain):
    pod_count = lax.axis_size("outer")
    width = tokens.shape[1]
    fast_total = summed_on_arrival(fast_weights[0], "outer", 1)
    slow_next, momentum_next = outer_update(slow_weights, momentum, fast_total, pod_count)
    fast_next = collect(slow_next, "outer", 1)
    values = tokens.astype(jnp.float32)
    meansq = jnp.mean(values * values, axis=-1, keepdims=True)
    normed = (values * lax.rsqrt(meansq + EPSILON) * norm_gain).astype(jnp.bfloat16)
    whole_weights = lax.all_gather(fast_next.astype(jnp.bfloat16), "dp", axis=0, tiled=True)
    product = jnp.dot(normed, whole_weights, preferred_element_type=jnp.float32)
    key_values = (product * width ** (-0.5)).astype(jnp.bfloat16)
    return (slow_next, momentum_next, fast_next, key_values)


def solution(mesh):
    in_specs = (
        P("outer", "dp", None),
        P("dp", "outer"),
        P("dp", "outer"),
        P(("outer", "dp"), None),
        P(),
    )
    out_specs = (P("dp", "outer"), P("dp", "outer"), P("dp", None), P(("outer", "dp"), None))
    return jax.shard_map(body, mesh=mesh, in_specs=in_specs, out_specs=out_specs, check_vma=False)
```

profile of v0, /device:TPU:17, one launch (start us, length us, event | category | flops | bytes accessed | tf_op | source)
XLA Modules:
  0.0 206.3 jit_solution(3373704709159486115)
XLA Ops:
  7.2 0.0 copy-start.1
  7.2 0.0 all-gather.2.cloned.1.call-start
  7.2 1.5 copy.9
  8.8 0.3 copy.10
  9.1 20.6 %all_to_all.10 = f32[8,128,256]{2,1,0:T(8,128)S(1)} all-to-all(f32[8,128,256]{2,1,0:T(8,128)S(1)} %copy.10), channel_id=1, replica_groups=mesh['outer'=8,'dp'=32] {'outer'}, dimensions={0} | all-to-all | bytes 2097152 | tf_op jit(solution)/shard_map/all_to_all | solution.py:18
  29.7 0.1 reduce_sum.18
  29.7 1.7 multiply_subtract_fusion
  31.4 0.0 copy-start
  31.4 0.1 broadcast_in_dim.2
  31.5 17.5 %all_to_all.11 = f32[8,128,256]{2,1,0:T(8,128)S(1)} all-to-all(f32[8,128,256]{2,1,0:T(8,128)S(1)} %broadcast_in_dim.2), channel_id=1, replica_groups=mesh['outer'=8,'dp'=32] {'outer'}, dimensions={0} | all-to-all | bytes 2097152 | tf_op jit(solution)/shard_map/all_to_all | solution.py:30
  49.0 0.3 copy.11
  49.3 0.9 bitcast_convert_fusion
  50.1 0.0 all-gather.2.cloned.1.call-update
  50.2 4.1 %fusion = f32[768]{0:T(1024)S(1)} fusion(bf16[768,4096]{1,0:T(8,128)(2,1)} %param.8), kind=kLoop, calls=%fused_computation.2 | loop fusion | flops 9436416 | bytes 6294528 | tf_op jit(solution)/shard_map/reduce_sum | solution.py:51
  54.3 1.3 copy.12
  55.6 124.2 %all-gather.2.cloned.1.call-done = bf16[4096,2048]{0,1:T(8,128)(2,1)} async-done(((bf16[128,2048]{0,1:T(8,128)(2,1)}), bf16[4096,2048]{0,1:T(8,128)(2,1)}) %all-gather.2.cloned.1.call-update) | async-done | bytes 16777232 | tf_op jit(solution)/shard_map/all_gather | solution.py:53
  179.7 0.0 copy-done.1
  179.7 19.7 %multiply_convert_fusion = bf16[768,2048]{1,0:T(8,128)(2,1)} fusion(bf16[4096,2048]{0,1:T(8,128)(2,1)} %all-gather.2.cloned.1.call-done, bf16[768,4096]{1,0:T(8,128)(2,1)} %param.8, f32[4096]{0:T(1024)S(1)} %copy-done.1, f32[768]{0:T(1024)S(1)} %add_rsqrt_fusion), kind=kOutput, calls=%fused_computation.6 | convolution fusion | flops 12900630528 | bytes 26233856 | tf_op jit(solution)/shard_map/dot_general | solution.py:54
  199.5 0.0 copy-done
  (1 shorter events, 0.0 us)
Async XLA Ops:
  7.2 172.6 %copy-start.1 = (f32[4096]{0:T(1024)S(1)}, f32[4096]{0:T(1024)}, u32[]{:S(2)}) copy-start(f32[4096]{0:T(1024)} %param.9) | copy-start | bytes 49156
  7.2 172.6 %all-gather.2.cloned.1.call-start = ((), (), s32[]{:S(2)}) async-start(), calls=%async_computation.2 | async-start | bytes 17301504 | tf_op jit(solution)/shard_map/all_gather | solution.py:53
  31.4 168.1 %copy-start = (f32[128,256]{1,0:T(8,128)}, f32[128,256]{1,0:T(8,128)S(1)}, u32[]{:S(2)}) copy-start(f32[128,256]{1,0:T(8,128)S(1)} %get-tuple-element.8) | copy-start | bytes 393220
Sparse Core Ops, SparseCore 0:
  50.3 129.4 all-gather.1
where the time goes:
time: 207 us; the launch traced here: 206 us
  waiting for transfers between devices  124 us (60%)
  blocking collectives  38 us (18%)
  matrix products  19.7 us (10%)
  between operations  14.1 us (7%)
  other arithmetic  6.66 us (3%)
  local copies, waits for them, and re-layouts  3.61 us (2%)
    all_gather x1, waiting for transfers between devices, body(): lax.all_gather(fast_next.astype(jnp.bfloat16), 'dp', axis=0, tiled=True)  124 us
    all_to_all x1, blocking collectives, summed_on_arrival(): lax.all_to_all(parts, axis, split_axis=0, concat_axis=0, tiled=True)  20.6 us
    dot_general x1, matrix products, body(): product = jnp.dot(normed, whole_weights, preferred_element_type=jnp.float32)  19.7 us
    all_to_all x1, blocking collectives, sent_to_all(): return lax.all_to_all(copies, axis, split_axis=0, concat_axis=0, tiled=True)  17.5 us
  transfers between devices with their start and end apart: 1, of which 1 were waited for; matrix products, arithmetic and copies ran while one was open for 3% of the time, Pallas kernels for 0%

commit v1 on v0

--- a/solution.py
+++ b/solution.py
@@ -50,7 +50,11 @@
     values = tokens.astype(jnp.float32)
     meansq = jnp.mean(values * values, axis=-1, keepdims=True)
     normed = (values * lax.rsqrt(meansq + EPSILON) * norm_gain).astype(jnp.bfloat16)
-    whole_weights = lax.all_gather(fast_next.astype(jnp.bfloat16), "dp", axis=0, tiled=True)
+    block = fast_next.astype(jnp.bfloat16)
+    count = lax.axis_size("dp")
+    blocks = jnp.stack([block for _ in range(count)])
+    blocks = lax.all_to_all(blocks, "dp", split_axis=0, concat_axis=0)
+    whole_weights = jnp.concatenate(blocks, axis=0)
     product = jnp.dot(normed, whole_weights, preferred_element_type=jnp.float32)
     key_values = (product * width ** (-0.5)).astype(jnp.bfloat16)
     return (slow_next, momentum_next, fast_next, key_values)

time: 207 us -> 454 us (2.19)
  the two profiles are of different devices: /device:TPU:17 before, /device:TPU:96 now
where the time goes in v1:
time: 454 us
  waiting for transfers between devices  367 us (81%)
  blocking collectives  42.3 us (9%)
  matrix products  19.7 us (4%)
  local copies, waits for them, and re-layouts  9.81 us (2%)
  starting transfers between devices  8.12 us (2%)
  other arithmetic  5.87 us (1%)
    all_to_all x1, waiting for transfers between devices, body(): blocks = lax.all_to_all(blocks, 'dp', split_axis=0, concat_axis=0)  367 us
    all_to_all x1, blocking collectives, summed_on_arrival(): lax.all_to_all(parts, axis, split_axis=0, concat_axis=0, tiled=True)  23.6 us
    dot_general x1, matrix products, body(): product = jnp.dot(normed, whole_weights, preferred_element_type=jnp.float32)  19.7 us
    all_to_all x1, blocking collectives, sent_to_all(): return lax.all_to_all(copies, axis, split_axis=0, concat_axis=0, tiled=True)  18.7 us
  transfers between devices with their start and end apart: 1, of which 1 were waited for; matrix products, arithmetic and copies ran while one was open for 1% of the time, Pallas kernels for 0%

profile of v1, /device:TPU:96, one launch (start us, length us, event | category | flops | bytes accessed | tf_op | source)
XLA Modules:
  0.0 454.0 jit_solution(14462484436557550798)
XLA Ops:
  0.6 1.5 copy.9
  2.2 0.3 copy.10
  2.5 23.6 %all_to_all.15 = f32[8,128,256]{2,1,0:T(8,128)S(1)} all-to-all(f32[8,128,256]{2,1,0:T(8,128)S(1)} %copy.10), channel_id=1, replica_groups=mesh['outer'=8,'dp'=32] {'outer'}, dimensions={0} | all-to-all | bytes 2097152 | tf_op jit(solution)/shard_map/all_to_all | solution.py:18
  26.1 0.1 reduce_sum.18
  26.2 1.7 multiply_subtract_fusion
  27.8 0.0 copy-start
  27.8 0.1 broadcast_in_dim.2
  27.9 18.7 %all_to_all.16 = f32[8,128,256]{2,1,0:T(8,128)S(1)} all-to-all(f32[8,128,256]{2,1,0:T(8,128)S(1)} %broadcast_in_dim.2), channel_id=1, replica_groups=mesh['outer'=8,'dp'=32] {'outer'}, dimensions={0} | all-to-all | bytes 2097152 | tf_op jit(solution)/shard_map/all_to_all | solution.py:30
  46.6 0.3 copy.11
  47.0 0.1 bitcast_convert_fusion
  47.0 0.2 copy.12
  47.2 6.0 %stack.2 = bf16[32,128,2048]{2,1,0:T(8,128)(2,1)} broadcast(bf16[128,2048]{1,0:T(8,128)(2,1)S(1)} %copy.12), dimensions={1,2} | broadcast | bytes 17301504 | tf_op jit(solution)/shard_map/stack | solution.py:55
  53.2 0.0 copy-done
  53.2 0.0 copy-start.1
  53.2 8.1 %all-to-all-start.2 = ((bf16[32,128,2048]{2,1,0:T(8,128)(2,1)}), bf16[32,128,2048]{2,1,0:T(8,128)(2,1)}, u32[]{:S(2)}, u32[]{:S(2)}) async-start(bf16[32,128,2048]{2,1,0:T(8,128)(2,1)} %stack.2), calls=%async_computation.2 | async-start | bytes 33554432 | tf_op jit(solution)/shard_map/all_to_all | solution.py:56
  61.4 4.1 fusion
  65.4 1.3 copy.13
  66.8 367.5 %all-to-all-done.2 = bf16[32,128,2048]{2,1,0:T(8,128)(2,1)} async-done(((bf16[32,128,2048]{2,1,0:T(8,128)(2,1)}), bf16[32,128,2048]{2,1,0:T(8,128)(2,1)}, u32[]{:S(2)}, u32[]{:S(2)}) %all-to-all-start.2) | async-done | bytes 16777248 | tf_op jit(solution)/shard_map/all_to_all | solution.py:56
  434.2 0.0 copy-done.1
  434.2 19.7 %multiply_convert_fusion = bf16[768,2048]{1,0:T(8,128)(2,1)} fusion(bf16[4096,2048]{1,0:T(8,128)(2,1)} %bitcast.5, bf16[768,4096]{1,0:T(8,128)(2,1)} %param.8, f32[4096]{0:T(1024)S(1)} %copy-done.1, f32[768]{0:T(1024)S(1)} %add_rsqrt_fusion), kind=kOutput, calls=%fused_computation.6 | convolution fusion | flops 12900630528 | bytes 26233856 | tf_op jit(solution)/shard_map/dot_general | solution.py:58
  (1 shorter events, 0.0 us)
Async XLA Ops:
  27.8 25.4 %copy-start = (f32[128,256]{1,0:T(8,128)}, f32[128,256]{1,0:T(8,128)S(1)}, u32[]{:S(2)}) copy-start(f32[128,256]{1,0:T(8,128)S(1)} %get-tuple-element.8) | copy-start | bytes 393220
  53.2 381.0 %copy-start.1 = (f32[4096]{0:T(1024)S(1)}, f32[4096]{0:T(1024)}, u32[]{:S(2)}) copy-start(f32[4096]{0:T(1024)} %param.9) | copy-start | bytes 49156
  53.2 381.0 %all-to-all-start.2 = ((bf16[32,128,2048]{2,1,0:T(8,128)(2,1)}), bf16[32,128,2048]{2,1,0:T(8,128)(2,1)}, u32[]{:S(2)}, u32[]{:S(2)}) async-start(bf16[32,128,2048]{2,1,0:T(8,128)(2,1)} %stack.2), calls=%async_computation.2 | async-start | bytes 33554432 | tf_op jit(solution)/shard_map/all_to_all | solution.py:56
